TPU v7x, 512 devices: a whole 4x4x16 slice. The times are simulated.
512 devices in a mesh: section: 8 (over x, core), dp: 32 (over z, y_lo), mp: 2 (over y_hi).
Axes of the slice: x: 4, y: 4 (y_hi: 2, y_lo: 2; y = y_hi * 2 + y_lo), z: 16, core: 2. Of those that a mesh axis runs over, the one named last changes fastest.
Arguments:
- layer_inputs: bfloat16 [8, 128, 4096], P('section', None, 'mp'), may hold values from -6 to 6
- pre_act: bfloat16 [8, 128, 8192], P('section', None, 'dp'), may hold values from -6 to 6
- out_grad: bfloat16 [128, 4096], P(None, 'mp'), may hold values from -4 to 4
- w_in: bfloat16 [32, 8, 32, 4096], P('dp', 'section', None, 'mp'), may hold values from -0.09375 to 0.09375
- w_out: bfloat16 [32, 8, 32, 4096], P('dp', 'section', None, 'mp'), may hold values from -0.0625 to 0.0625
Outputs:
- in_grads: bfloat16 [8, 128, 4096], P('section', None, 'mp')
- grad_in: float32 [32, 8, 32, 4096], P('dp', 'section', None, 'mp')
- grad_out: float32 [32, 8, 32, 4096], P('dp', 'section', None, 'mp')
All inputs are finite; a program needn't handle non-finite values.
Results may differ from a plain program's by a relative error of at most 0.035.
Values may be sent and summed in bfloat16 or wider, within the bound.
No kernel may reach another device: no remote copies, remote signals or barrier semaphores. Data moves between devices by JAX's collectives and lax.ppermute only.
A program may use at most 64 MiB of HBM per device.

v0:
```python
import jax
import jax.numpy as jnp
from jax import lax
from jax.sharding import Mesh
from jax.sharding import PartitionSpec as P

MICRO = 2
DP = ("dp_0", "dp_1")


def sent_together(arrays, axis, dim, along):
    both = jnp.concatenate(arrays, axis=along)
    result, at, outs = (lax.all_gather(both, axis, axis=dim, tiled=True), 0, [])
    for a in arrays:
        outs.append(lax.slice_in_dim(result, at, at + a.shape[along], axis=along))
        at += a.shape[along]
    return tuple(outs)


def over_pieces(value, axis):
    return lax.all_gather(value, axis).astype(jnp.float32).sum(0)


def over_axes(value, axes):
    for axis in axes:
        value = lax.psum(value, axis)
    return value


def shifted(value, axis, by):
    size = lax.axis_size(axis)
    pairs = [(i, i + by) for i in range(size) if 0 <= i + by < size]
    return lax.ppermute(value, axis, pairs)


def in_one_piece(arrays, axis, dim, along):
    ends, at = ([], 0)
    for a in arrays[:-1]:
        at += a.shape[along]
        ends.append(at)
    both = jnp.concatenate(arrays, axis=along)
    return tuple(
        jnp.split(lax.psum_scatter(both, axis, scatter_dimension=dim, tiled=True), ends, axis=along)
    )


def gelu_slope(value):
    cdf = 0.5 * (1.0 + lax.erf(value * 0.7071067811865476))
    dens = jnp.exp(-0.5 * value * value) * 0.3989422804014327
    return cdf + value * dens


def by_tokens(left, right):
    return lax.dot_general(
        left, right, (((0,), (0,)), ((), ())), preferred_element_type=jnp.float32
    )


def body(layer_inputs, pre_act, out_grad, w_in, w_out):
    sections = lax.axis_size("section")
    spot = lax.axis_index("section")
    tok_rows = out_grad.shape[0]
    block = tok_rows // MICRO
    width = out_grad.shape[1]
    full_in, full_out = sent_together((w_in, w_out), "section", 1, 0)
    units = full_in.shape[1] * full_in.shape[2]
    per_block = full_in.shape[2]
    in_rows = full_in.reshape(units, width)
    out_rows = full_out.reshape(units, width)
    inputs = layer_inputs[0]
    saved = pre_act[0]
    is_last = spot == sections - 1

    def advance(step, state):
        incoming, dys, gees, results = state
        micro_id = step - (sections - 1 - spot)
        valid = jnp.logical_and(micro_id >= 0, micro_id < MICRO)
        begin = jnp.clip(micro_id, 0, MICRO - 1) * block
        given = lax.dynamic_slice_in_dim(out_grad, begin, block, 0)
        upper = jnp.where(is_last, given, incoming)
        partial_value = lax.dot_general(
            upper, out_rows, (((1,), (1,)), ((), ())), preferred_element_type=jnp.float32
        )
        summed = over_pieces(partial_value.astype(jnp.bfloat16), "mp").astype(jnp.float32)
        rows_pre = lax.dynamic_slice_in_dim(saved, begin, block, 0).astype(jnp.float32)
        gee = (summed * gelu_slope(rows_pre)).astype(jnp.bfloat16)
        branch = jnp.dot(gee, in_rows, preferred_element_type=jnp.float32)
        total = over_axes(branch.astype(jnp.bfloat16), DP).astype(jnp.float32)
        result = (upper.astype(jnp.float32) + total).astype(jnp.bfloat16)
        outgoing = shifted(result, "section", -1)
        old_dy = lax.dynamic_slice_in_dim(dys, begin, block, 0)
        old_gee = lax.dynamic_slice_in_dim(gees, begin, block, 0)
        old_res = lax.dynamic_slice_in_dim(results, begin, block, 0)
        dys = lax.dynamic_update_slice_in_dim(dys, jnp.where(valid, upper, old_dy), begin, 0)
        gees = lax.dynamic_update_slice_in_dim(gees, jnp.where(valid, gee, old_gee), begin, 0)
        results = lax.dynamic_update_slice_in_dim(
            results, jnp.where(valid, result, old_res), begin, 0
        )
        return (outgoing, dys, gees, results)

    start_state = (
        jnp.zeros((block, width), jnp.bfloat16),
        jnp.zeros((tok_rows, width), jnp.bfloat16),
        jnp.zeros((tok_rows, units), jnp.bfloat16),
        jnp.zeros((tok_rows, width), jnp.bfloat16),
    )
    final_state = lax.fori_loop(0, sections + MICRO - 1, advance, start_state)
    dys = final_state[1]
    gees = final_state[2]
    results = final_state[3]
    hidden = jax.nn.gelu(saved.astype(jnp.float32), approximate=False).astype(jnp.bfloat16)
    term_in = by_tokens(gees, inputs).reshape(1, sections, per_block, width)
    term_out = by_tokens(hidden, dys).reshape(1, sections, per_block, width)
    grad_in, grad_out = tuple(
        (
            part.astype(jnp.float32)
            for part in in_one_piece(
                (term_in.astype(jnp.bfloat16), term_out.astype(jnp.bfloat16)), "section", 1, 0
            )
        )
    )
    return (results[None], grad_in, grad_out)


def solution(mesh):
    split = Mesh(
        mesh.devices.reshape(mesh.shape["section"], 16, 2, mesh.shape["mp"]),
        ("section", "dp_0", "dp_1", "mp"),
    )
    placed = (
        P("section", None, "mp"),
        P("section", None, DP),
        P(None, "mp"),
        P(DP, "section", None, "mp"),
        P(DP, "section", None, "mp"),
    )
    return jax.shard_map(
        body,
        mesh=split,
        in_specs=placed,
        out_specs=(
            P("section", None, "mp"),
            P(DP, "section", None, "mp"),
            P(DP, "section", None, "mp"),
        ),
        check_vma=False,
    )
```

profile of v0, /device:TPU:8, one launch (start us, length us, event | category | flops | bytes accessed | tf_op | source)
XLA Modules:
  0.0 1952.7 jit_solution(7781573785871670471)
XLA Ops:
  10.9 37.2 %all-gather.5.cloned.1.call-done = bf16[2,8,32,2048]{3,2,1,0:T(8,128)(2,1)} async-done(((bf16[2,1,32,2048]{3,2,1,0:T(8,128)(2,1)}), bf16[2,8,32,2048]{3,2,1,0:T(8,128)(2,1)}) %all-gather.5.cloned.1.call-update) | async-done | bytes 2097168 | tf_op jit(solution)/shard_map/all_gather | solution.py:13
  52.0 1801.6 %while.21 = (s32[]{:T(128)}, bf16[64,2048]{1,0:T(8,128)(2,1)}, bf16[128,2048]{1,0:T(8,128)(2,1)S(1)}, bf16[128,256]{1,0:T(8,128)(2,1)}, bf16[128,2048]{1,0:T(8,1...) while((s32[]{:T(128)}, bf16[64,2048]{1,0:T(8,128)(2,1)}, ...), condition=%wide.region_4.5_spmd, body=%wide.region_0.4_spmd.sunk | while | flops 135970816 | bytes 11010468 | solution.py:107
  53.6 6.1 all-gather.2
  60.8 137.2 %all-reduce.7.cloned.1.call-done = bf16[64,2048]{1,0:T(8,128)(2,1)} async-done(((bf16[64,2048]{1,0:T(8,128)(2,1)}), bf16[64,2048]{1,0:T(8,128)(2,1)}) %all-reduce.7.cloned.1.call-update) | async-done | bytes 262160 | tf_op jit(solution)/shard_map/while/body/eval_jaxpr/psum | solution.py:26
  198.0 45.2 %all-reduce.9.cloned.1.call-done = bf16[64,2048]{1,0:T(8,128)(2,1)} async-done(((bf16[64,2048]{1,0:T(8,128)(2,1)}), bf16[64,2048]{1,0:T(8,128)(2,1)}) %all-reduce.9.cloned.1.call-update) | async-done | bytes 262160 | tf_op jit(solution)/shard_map/while/body/eval_jaxpr/psum | solution.py:26
  243.2 1.9 select_dynamic-update-slice_fusion.7
  251.1 6.1 all-gather.2
  258.3 140.3 %all-reduce.7.cloned.1.call-done = bf16[64,2048]{1,0:T(8,128)(2,1)} async-done(((bf16[64,2048]{1,0:T(8,128)(2,1)}), bf16[64,2048]{1,0:T(8,128)(2,1)}) %all-reduce.7.cloned.1.call-update) | async-done | bytes 262160 | tf_op jit(solution)/shard_map/while/body/eval_jaxpr/psum | solution.py:26
  398.6 45.1 %all-reduce.9.cloned.1.call-done = bf16[64,2048]{1,0:T(8,128)(2,1)} async-done(((bf16[64,2048]{1,0:T(8,128)(2,1)}), bf16[64,2048]{1,0:T(8,128)(2,1)}) %all-reduce.9.cloned.1.call-update) | async-done | bytes 262160 | tf_op jit(solution)/shard_map/while/body/eval_jaxpr/psum | solution.py:26
  451.5 6.1 all-gather.2
  458.7 140.3 %all-reduce.7.cloned.1.call-done = bf16[64,2048]{1,0:T(8,128)(2,1)} async-done(((bf16[64,2048]{1,0:T(8,128)(2,1)}), bf16[64,2048]{1,0:T(8,128)(2,1)}) %all-reduce.7.cloned.1.call-update) | async-done | bytes 262160 | tf_op jit(solution)/shard_map/while/body/eval_jaxpr/psum | solution.py:26
  599.0 45.2 %all-reduce.9.cloned.1.call-done = bf16[64,2048]{1,0:T(8,128)(2,1)} async-done(((bf16[64,2048]{1,0:T(8,128)(2,1)}), bf16[64,2048]{1,0:T(8,128)(2,1)}) %all-reduce.9.cloned.1.call-update) | async-done | bytes 262160 | tf_op jit(solution)/shard_map/while/body/eval_jaxpr/psum | solution.py:26
  652.1 6.1 all-gather.2
  659.3 140.3 %all-reduce.7.cloned.1.call-done = bf16[64,2048]{1,0:T(8,128)(2,1)} async-done(((bf16[64,2048]{1,0:T(8,128)(2,1)}), bf16[64,2048]{1,0:T(8,128)(2,1)}) %all-reduce.7.cloned.1.call-update) | async-done | bytes 262160 | tf_op jit(solution)/shard_map/while/body/eval_jaxpr/psum | solution.py:26
  799.6 45.2 %all-reduce.9.cloned.1.call-done = bf16[64,2048]{1,0:T(8,128)(2,1)} async-done(((bf16[64,2048]{1,0:T(8,128)(2,1)}), bf16[64,2048]{1,0:T(8,128)(2,1)}) %all-reduce.9.cloned.1.call-update) | async-done | bytes 262160 | tf_op jit(solution)/shard_map/while/body/eval_jaxpr/psum | solution.py:26
  852.7 6.1 all-gather.2
  859.9 140.3 %all-reduce.7.cloned.1.call-done = bf16[64,2048]{1,0:T(8,128)(2,1)} async-done(((bf16[64,2048]{1,0:T(8,128)(2,1)}), bf16[64,2048]{1,0:T(8,128)(2,1)}) %all-reduce.7.cloned.1.call-update) | async-done | bytes 262160 | tf_op jit(solution)/shard_map/while/body/eval_jaxpr/psum | solution.py:26
  1000.1 45.2 %all-reduce.9.cloned.1.call-done = bf16[64,2048]{1,0:T(8,128)(2,1)} async-done(((bf16[64,2048]{1,0:T(8,128)(2,1)}), bf16[64,2048]{1,0:T(8,128)(2,1)}) %all-reduce.9.cloned.1.call-update) | async-done | bytes 262160 | tf_op jit(solution)/shard_map/while/body/eval_jaxpr/psum | solution.py:26
  1053.3 6.1 all-gather.2
  1060.4 140.3 %all-reduce.7.cloned.1.call-done = bf16[64,2048]{1,0:T(8,128)(2,1)} async-done(((bf16[64,2048]{1,0:T(8,128)(2,1)}), bf16[64,2048]{1,0:T(8,128)(2,1)}) %all-reduce.7.cloned.1.call-update) | async-done | bytes 262160 | tf_op jit(solution)/shard_map/while/body/eval_jaxpr/psum | solution.py:26
  1200.7 45.2 %all-reduce.9.cloned.1.call-done = bf16[64,2048]{1,0:T(8,128)(2,1)} async-done(((bf16[64,2048]{1,0:T(8,128)(2,1)}), bf16[64,2048]{1,0:T(8,128)(2,1)}) %all-reduce.9.cloned.1.call-update) | async-done | bytes 262160 | tf_op jit(solution)/shard_map/while/body/eval_jaxpr/psum | solution.py:26
  1253.8 6.1 all-gather.2
  1261.0 140.3 %all-reduce.7.cloned.1.call-done = bf16[64,2048]{1,0:T(8,128)(2,1)} async-done(((bf16[64,2048]{1,0:T(8,128)(2,1)}), bf16[64,2048]{1,0:T(8,128)(2,1)}) %all-reduce.7.cloned.1.call-update) | async-done | bytes 262160 | tf_op jit(solution)/shard_map/while/body/eval_jaxpr/psum | solution.py:26
  1401.3 45.1 %all-reduce.9.cloned.1.call-done = bf16[64,2048]{1,0:T(8,128)(2,1)} async-done(((bf16[64,2048]{1,0:T(8,128)(2,1)}), bf16[64,2048]{1,0:T(8,128)(2,1)}) %all-reduce.9.cloned.1.call-update) | async-done | bytes 262160 | tf_op jit(solution)/shard_map/while/body/eval_jaxpr/psum | solution.py:26
  1454.2 6.1 all-gather.2
  1461.4 140.3 %all-reduce.7.cloned.1.call-done = bf16[64,2048]{1,0:T(8,128)(2,1)} async-done(((bf16[64,2048]{1,0:T(8,128)(2,1)}), bf16[64,2048]{1,0:T(8,128)(2,1)}) %all-reduce.7.cloned.1.call-update) | async-done | bytes 262160 | tf_op jit(solution)/shard_map/while/body/eval_jaxpr/psum | solution.py:26
  1601.7 45.1 %all-reduce.9.cloned.1.call-done = bf16[64,2048]{1,0:T(8,128)(2,1)} async-done(((bf16[64,2048]{1,0:T(8,128)(2,1)}), bf16[64,2048]{1,0:T(8,128)(2,1)}) %all-reduce.9.cloned.1.call-update) | async-done | bytes 262160 | tf_op jit(solution)/shard_map/while/body/eval_jaxpr/psum | solution.py:26
  1654.7 6.1 all-gather.2
  1661.8 140.3 %all-reduce.7.cloned.1.call-done = bf16[64,2048]{1,0:T(8,128)(2,1)} async-done(((bf16[64,2048]{1,0:T(8,128)(2,1)}), bf16[64,2048]{1,0:T(8,128)(2,1)}) %all-reduce.7.cloned.1.call-update) | async-done | bytes 262160 | tf_op jit(solution)/shard_map/while/body/eval_jaxpr/psum | solution.py:26
  1802.1 45.2 %all-reduce.9.cloned.1.call-done = bf16[64,2048]{1,0:T(8,128)(2,1)} async-done(((bf16[64,2048]{1,0:T(8,128)(2,1)}), bf16[64,2048]{1,0:T(8,128)(2,1)}) %all-reduce.9.cloned.1.call-update) | async-done | bytes 262160 | tf_op jit(solution)/shard_map/while/body/eval_jaxpr/psum | solution.py:26
  1859.1 84.4 %all-reduce.5.cloned.1.call-done = bf16[2,8,32,2048]{3,2,1,0:T(8,128)(2,1)} async-done(((bf16[2,8,32,2048]{3,2,1,0:T(8,128)(2,1)}), bf16[2,8,32,2048]{3,2,1,0:T(8,128)(2,1)}) %all-reduce.5.cloned.1.call-update) | async-done | bytes 2097168
  1943.5 2.4 dynamic-slice_convert_fusion
  (146 shorter events, 91.6 us)
Async XLA Ops:
  7.2 1848.7 %copy-start = (bf16[1,128,2048]{2,1,0:T(8,128)(2,1)S(1)}, bf16[1,128,2048]{2,1,0:T(8,128)(2,1)}, u32[]{:S(2)}) copy-start(bf16[1,128,2048]{2,1,0:T(8,128)(2,1)} %param.7) | copy-start | bytes 1572868
  7.2 40.9 %all-gather.5.cloned.1.call-start = ((), (), s32[]{:S(2)}) async-start(), calls=%async_computation | async-start | bytes 2359296 | tf_op jit(solution)/shard_map/all_gather | solution.py:13
  10.9 41.1 %copy-start.2 = (bf16[1,128,256]{2,1,0:T(8,128)(2,1)S(1)}, bf16[1,128,256]{2,1,0:T(8,128)(2,1)}, u32[]{:S(2)}) copy-start(bf16[1,128,256]{2,1,0:T(8,128)(2,1)} %param.8) | copy-start | bytes 196612
  52.0 146.0 %all-reduce.7.cloned.1.call-start = ((), (), s32[]{:S(2)}) async-start(), calls=%async_computation.2 | async-start | bytes 524288 | tf_op jit(solution)/shard_map/while/body/eval_jaxpr/psum | solution.py:26
  60.7 182.5 %all-reduce.9.cloned.1.call-start = ((), (), s32[]{:S(2)}) async-start(), calls=%async_computation.3 | async-start | bytes 524288 | tf_op jit(solution)/shard_map/while/body/eval_jaxpr/psum | solution.py:26
  245.2 3.6 collective-permute-start
  249.5 149.0 %all-reduce.7.cloned.1.call-start = ((), (), s32[]{:S(2)}) async-start(), calls=%async_computation.2 | async-start | bytes 524288 | tf_op jit(solution)/shard_map/while/body/eval_jaxpr/psum | solution.py:26
  258.3 185.4 %all-reduce.9.cloned.1.call-start = ((), (), s32[]{:S(2)}) async-start(), calls=%async_computation.3 | async-start | bytes 524288 | tf_op jit(solution)/shard_map/while/body/eval_jaxpr/psum | solution.py:26
  445.6 3.6 collective-permute-start
  449.9 149.0 %all-reduce.7.cloned.1.call-start = ((), (), s32[]{:S(2)}) async-start(), calls=%async_computation.2 | async-start | bytes 524288 | tf_op jit(solution)/shard_map/while/body/eval_jaxpr/psum | solution.py:26
  458.7 185.6 %all-reduce.9.cloned.1.call-start = ((), (), s32[]{:S(2)}) async-start(), calls=%async_computation.3 | async-start | bytes 524288 | tf_op jit(solution)/shard_map/while/body/eval_jaxpr/psum | solution.py:26
  646.2 3.6 collective-permute-start
  649.8 0.7 copy-start.1
  650.5 149.0 %all-reduce.7.cloned.1.call-start = ((), (), s32[]{:S(2)}) async-start(), calls=%async_computation.2 | async-start | bytes 524288 | tf_op jit(solution)/shard_map/while/body/eval_jaxpr/psum | solution.py:26
  659.2 185.6 %all-reduce.9.cloned.1.call-start = ((), (), s32[]{:S(2)}) async-start(), calls=%async_computation.3 | async-start | bytes 524288 | tf_op jit(solution)/shard_map/while/body/eval_jaxpr/psum | solution.py:26
  846.7 3.6 collective-permute-start
  851.1 149.0 %all-reduce.7.cloned.1.call-start = ((), (), s32[]{:S(2)}) async-start(), calls=%async_computation.2 | async-start | bytes 524288 | tf_op jit(solution)/shard_map/while/body/eval_jaxpr/psum | solution.py:26
  859.8 185.6 %all-reduce.9.cloned.1.call-start = ((), (), s32[]{:S(2)}) async-start(), calls=%async_computation.3 | async-start | bytes 524288 | tf_op jit(solution)/shard_map/while/body/eval_jaxpr/psum | solution.py:26
  1047.3 3.6 collective-permute-start
  1051.7 149.0 %all-reduce.7.cloned.1.call-start = ((), (), s32[]{:S(2)}) async-start(), calls=%async_computation.2 | async-start | bytes 524288 | tf_op jit(solution)/shard_map/while/body/eval_jaxpr/psum | solution.py:26
  1060.4 185.6 %all-reduce.9.cloned.1.call-start = ((), (), s32[]{:S(2)}) async-start(), calls=%async_computation.3 | async-start | bytes 524288 | tf_op jit(solution)/shard_map/while/body/eval_jaxpr/psum | solution.py:26
  1247.9 3.6 collective-permute-start
  1252.2 149.0 %all-reduce.7.cloned.1.call-start = ((), (), s32[]{:S(2)}) async-start(), calls=%async_computation.2 | async-start | bytes 524288 | tf_op jit(solution)/shard_map/while/body/eval_jaxpr/psum | solution.py:26
  1261.0 185.4 %all-reduce.9.cloned.1.call-start = ((), (), s32[]{:S(2)}) async-start(), calls=%async_computation.3 | async-start | bytes 524288 | tf_op jit(solution)/shard_map/while/body/eval_jaxpr/psum | solution.py:26
  1448.3 3.6 collective-permute-start
  1452.6 149.0 %all-reduce.7.cloned.1.call-start = ((), (), s32[]{:S(2)}) async-start(), calls=%async_computation.2 | async-start | bytes 524288 | tf_op jit(solution)/shard_map/while/body/eval_jaxpr/psum | solution.py:26
  1461.4 185.4 %all-reduce.9.cloned.1.call-start = ((), (), s32[]{:S(2)}) async-start(), calls=%async_computation.3 | async-start | bytes 524288 | tf_op jit(solution)/shard_map/while/body/eval_jaxpr/psum | solution.py:26
  1648.7 3.6 collective-permute-start
  1653.1 149.0 %all-reduce.7.cloned.1.call-start = ((), (), s32[]{:S(2)}) async-start(), calls=%async_computation.2 | async-start | bytes 524288 | tf_op jit(solution)/shard_map/while/body/eval_jaxpr/psum | solution.py:26
  1661.8 185.6 %all-reduce.9.cloned.1.call-start = ((), (), s32[]{:S(2)}) async-start(), calls=%async_computation.3 | async-start | bytes 524288 | tf_op jit(solution)/shard_map/while/body/eval_jaxpr/psum | solution.py:26
  1849.3 3.6 collective-permute-start
  1853.6 89.8 %all-reduce.5.cloned.1.call-start = ((), (), s32[]{:S(2)}) async-start(), calls=%async_computation.1 | async-start | bytes 4194304
  (8 other events, 5.6 us)
Sparse Core Ops, SparseCore 0:
  10.7 37.3 all-gather.4
  60.9 137.0 all-reduce.6
  200.9 42.3 all-reduce.8
  258.4 140.1 all-reduce.6
  401.3 42.3 all-reduce.8
  458.8 140.1 all-reduce.6
  601.8 42.3 all-reduce.8
  659.4 140.1 all-reduce.6
  802.4 42.3 all-reduce.8
  859.9 140.1 all-reduce.6
  1003.0 42.3 all-reduce.8
  1060.5 140.1 all-reduce.6
  1203.6 42.3 all-reduce.8
  1261.1 140.1 all-reduce.6
  1404.0 42.3 all-reduce.8
  1461.5 140.1 all-reduce.6
  1604.4 42.3 all-reduce.8
  1661.9 140.1 all-reduce.6
  1805.0 42.3 all-reduce.8
  1857.9 85.4 all-reduce.4
where the time goes:
time: 1950 us
  waiting for transfers between devices  1800 us (92%)
  blocking collectives  54.8 us (3%)
  other arithmetic  47.1 us (2%)
    psum x18, waiting for transfers between devices, over_axes(): value = lax.psum(value, axis)  1670 us
    unnamed x3, waiting for transfers between devices  84.4 us
    all_gather x9, blocking collectives, over_pieces(): return lax.all_gather(value, axis).astype(jnp.float32).sum(0)  54.8 us
  transfers between devices with their start and end apart: 29, of which 29 were waited for; matrix products, arithmetic and copies ran while one was open for 1% of the time, Pallas kernels for 0%

commit v1 on v0

v1 whole, which is shorter than its diff:
```python
import jax
import jax.numpy as jnp
from jax import lax
from jax.sharding import Mesh
from jax.sharding import PartitionSpec as P

F32 = jnp.float32
BF16 = jnp.bfloat16
SEC = ("x", "core")
DP = ("z", "yl")
TOK = ("z", "core")
ROWS = ("x", "yl")


def size(axes):
    n = 1
    for a in axes:
        n *= lax.axis_size(a)
    return n


def shared(value, axes):
    n = size(axes)
    return lax.all_to_all(
        jnp.broadcast_to(value[None], (n,) + value.shape), axes, 0, 0, tiled=True
    )


def gelu_slope(value):
    cdf = 0.5 * (1.0 + lax.erf(value * 0.7071067811865476))
    dens = jnp.exp(-0.5 * value * value) * 0.3989422804014327
    return cdf + value * dens


def dot(left, right, dims):
    return lax.dot_general(left, right, (dims, ((), ())), preferred_element_type=F32)


def body(layer_inputs, pre_act, out_grad, w_in, w_out):
    nx, nc, nz, nyl = (lax.axis_size(a) for a in ("x", "core", "z", "yl"))
    sections, groups = nx * nc, nz * nc
    tok_rows, width = out_grad.shape
    per = w_in.shape[2]
    each = tok_rows // groups
    units = groups * per
    own_in = w_in.reshape(per, width)
    own_out = w_out.reshape(per, width)
    saved = pre_act[0]
    spot = lax.axis_index(SEC)
    mine = lax.axis_index(TOK)

    both = lax.all_gather(jnp.concatenate([own_out, own_in], 0), TOK, axis=0)
    rows_out = both[:, :per].reshape(units, width)
    rows_in = both[:, per:].reshape(units, width)
    inputs = lax.all_gather(layer_inputs[0], SEC, axis=0)

    own_pre = lax.all_to_all(
        saved.reshape(tok_rows, sections, per).transpose(1, 0, 2), SEC, 0, 0, tiled=True
    ).astype(F32)
    part = dot(out_grad, own_out, ((1,), (1,))).astype(BF16)
    back = lax.all_gather(part, "mp").astype(F32).sum(0)
    gee_last = (back * gelu_slope(own_pre[sections - 1])).astype(BF16)
    gee = lax.all_to_all(gee_last.reshape(groups, each, per), TOK, 0, 0, tiled=True)
    gee = gee.transpose(1, 0, 2).reshape(each, units)
    sent = saved.reshape(nz, nc, each, nx, nc, per).transpose(3, 1, 0, 2, 4, 5)
    sent = sent.reshape(nx * nc * nz, each * nc * per // 128, 128)
    got = lax.all_to_all(sent, ("x", "core", "z"), 0, 0, tiled=True)
    got = got.reshape(sections, nz, each, nc, per).transpose(0, 2, 1, 3, 4)
    slopes = gelu_slope(got.reshape(sections, each, units).astype(F32))

    upper = lax.dynamic_slice_in_dim(out_grad, mine * each, each, 0)
    gees, results = [], []
    for s in reversed(range(sections)):
        if s < sections - 1:
            part = dot(upper, rows_out, ((1,), (1,))).astype(BF16)
            back = lax.all_gather(part, "mp").astype(F32).sum(0)
            gee = (back * slopes[s]).astype(BF16)
            gees.append(gee)
        branch = dot(gee, rows_in, ((1,), (0,))).astype(BF16)
        total = shared(branch, ROWS).astype(F32).sum(0)
        upper = (upper.astype(F32) + total).astype(BF16)
        results.append(upper)
    early = jnp.concatenate(results[: sections - 2], 0)
    early = lax.all_gather(early, TOK, axis=0).reshape(groups, sections - 2, each, width)
    late = []
    for r in results[sections - 2 :]:
        r = shared(r, ("z",))
        r = lax.all_gather(r, "core", axis=1)
        late.append(r.reshape(groups, 1, each, width))
    grads = jnp.concatenate([early] + late, 1)

    gs = jnp.stack(gees, 0).reshape(sections - 1, each, groups, per).transpose(2, 0, 1, 3)
    gs = lax.all_to_all(gs.reshape(groups, -1, 128), TOK, 0, 0, tiled=True)
    gs = gs.reshape(groups, sections - 1, each, per).transpose(1, 0, 2, 3)
    gs = jnp.concatenate([gee_last[None], gs.reshape(sections - 1, tok_rows, per)], 0)[::-1]
    grad_in = dot(
        gs.reshape(sections * tok_rows, per),
        inputs.reshape(sections * tok_rows, width),
        ((0,), (0,)),
    )
    hidden = jax.nn.gelu(own_pre, approximate=False).astype(BF16)
    low = hidden[: sections - 1][::-1].reshape(sections - 1, groups, each, per)
    low = low.transpose(1, 0, 2, 3).reshape(-1, per)
    grad_out = dot(hidden[sections - 1], out_grad, ((0,), (0,))) + dot(
        low, grads[:, : sections - 1].reshape(-1, width), ((0,), (0,))
    )
    in_grads = lax.dynamic_index_in_dim(grads, sections - 1 - spot, 1, False)
    return (
        in_grads.reshape(1, tok_rows, width),
        grad_in.reshape(w_in.shape),
        grad_out.reshape(w_out.shape),
    )


def solution(mesh):
    split = Mesh(
        mesh.devices.reshape(
            mesh.shape["section"] // 2, 2, mesh.shape["dp"] // 2, 2, mesh.shape["mp"]
        ),
        ("x", "core", "z", "yl", "mp"),
    )
    placed = (
        P(SEC, None, "mp"),
        P(SEC, None, DP),
        P(None, "mp"),
        P(DP, SEC, None, "mp"),
        P(DP, SEC, None, "mp"),
    )
    return jax.shard_map(
        body,
        mesh=split,
        in_specs=placed,
        out_specs=(P(SEC, None, "mp"), P(DP, SEC, None, "mp"), P(DP, SEC, None, "mp")),
        check_vma=False,
    )
```

time: 1950 us -> 347 us (0.18)
  waiting for transfers between devices: 1800 us -> 92.7 us
  blocking collectives: 54.8 us -> 112 us
  starting transfers between devices: 12 us -> 55.7 us
  other arithmetic: 47.1 us -> 7.34 us
    psum x18 -> x0, waiting for transfers between devices: 1670 us -> none  [over_axes(): value = lax.psum(value, axis)]
    unnamed x3, waiting for transfers between devices: 84.4 us -> 0.59 us
    all_to_all x0 -> x9, waiting for transfers between devices: none -> 66.2 us  [the longest x6 43.1 us: shared(): lax.all_to_all(jnp.broadcast_to(value[None], (n,) + value.shape), axes, 0...]
    all_to_all x0 -> x5, blocking collectives: none -> 60.1 us  [the longest x4 38 us: shared(): lax.all_to_all(jnp.broadcast_to(value[None], (n,) + value.shape), axes, 0...]
    all_to_all x0 -> x9, starting transfers between devices: none -> 55.6 us  [the longest x6 29.5 us: shared(): lax.all_to_all(jnp.broadcast_to(value[None], (n,) + value.shape), axes, 0...]
    dynamic_update_slice x27 -> x0, other arithmetic: 40.5 us -> none  [the longest x9 17.4 us: advance(): lax.dynamic_update_slice_in_dim(results, jnp.where(valid, result, old_res...]
    all_gather x9 -> x10, blocking collectives: 54.8 us -> 51.5 us  [the longest x8 47.1 us: body(): back = lax.all_gather(part, 'mp').astype(F32).sum(0)]
  transfers between devices with their start and end apart: 29 -> 12, of which waited for: 29 -> 9; matrix products, arithmetic and copies ran while one was open for 1% -> 14% of each run, Pallas kernels for 0% -> 0%
where the time goes in v1:
time: 347 us; the launch traced here: 346 us
  blocking collectives  112 us (32%)
  waiting for transfers between devices  92.7 us (27%)
  starting transfers between devices  55.7 us (16%)
  matrix products  31.8 us (9%)
  local copies, waits for them, and re-layouts  30.4 us (9%)
  between operations  16 us (5%)
  other arithmetic  7.34 us (2%)
    all_gather x8, blocking collectives, body(): back = lax.all_gather(part, 'mp').astype(F32).sum(0)  47.1 us
    all_to_all x6, waiting for transfers between devices, shared(): lax.all_to_all(jnp.broadcast_to(value[None], (n,) + value.shape), axes, 0...  43.1 us
    all_to_all x4, blocking collectives, shared(): lax.all_to_all(jnp.broadcast_to(value[None], (n,) + value.shape), axes, 0...  38 us
    dot_general x19, matrix products, dot(): lax.dot_general(left, right, (dims, ((), ())), preferred_element_type=F32)  31.8 us
    all_to_all x6, starting transfers between devices, shared(): lax.all_to_all(jnp.broadcast_to(value[None], (n,) + value.shape), axes, 0...  29.5 us
    all_gather x1, waiting for transfers between devices, body(): both = lax.all_gather(jnp.concatenate([own_out, own_in], 0), TOK, axis=0)  26 us
    all_to_all x1, blocking collectives, body(): gs = lax.all_to_all(gs.reshape(groups, -1, 128), TOK, 0, 0, tiled=True)  22.1 us
    all_to_all x1, starting transfers between devices, body(): got = lax.all_to_all(sent, ('x', 'core', 'z'), 0, 0, tiled=True)  17.9 us
  transfers between devices with their start and end apart: 12, of which 9 were waited for; matrix products, arithmetic and copies ran while one was open for 14% of the time, Pallas kernels for 0%

profile of v1, /device:TPU:8, one launch (start us, length us, event | category | flops | bytes accessed | tf_op | source)
XLA Modules:
  0.0 345.6 jit_solution(6710467483781021386)
XLA Ops:
  11.3 4.3 %all-to-all-start = ((bf16[8,128,32]{1,2,0:T(8,128)(2,1)}), bf16[8,128,32]{1,2,0:T(8,128)(2,1)S(1)}, u32[]{:S(2)}, u32[]{:S(2)}) async-start(bf16[8,128,32]{1,2,0:T(8,128)(2,1)} %bitcast.3), calls=%async_computation | async-start | bytes 131072 | tf_op jit(solution)/shard_map/all_to_all | solution.py:57
  21.3 17.9 %all-to-all-start.3 = ((bf16[128,2,128]{2,1,0:T(2,128)(2,1)}), bf16[128,2,128]{2,1,0:T(2,128)(2,1)S(1)}, u32[]{:S(2)}, u32[]{:S(2)}) async-start(bf16[128,2,128]{2,1,0:T(2,128)(2,1)} %reshape.109), calls=%async_computation.3 | async-start | bytes 131072 | tf_op jit(solution)/shard_map/all_to_all | solution.py:67
  40.5 5.9 %all-gather = bf16[256,32]{0,1:T(8,128)(2,1)S(1)} all-gather(bf16[128,32]{0,1:T(8,128)(2,1)S(1)} %convolution_convert_fusion.14), channel_id=2, replica_groups=mesh['x'=4,'core'=2,'z'=16,'yl'=2,'mp'=2] {'mp'}, dimensions={0}, use_global_device_ids=true | all-gather | bytes 24576 | tf_op jit(solution)/shard_map/all_gather | solution.py:61
  47.3 7.6 %all-to-all-done.3 = bf16[128,2,128]{2,1,0:T(2,128)(2,1)S(1)} async-done(((bf16[128,2,128]{2,1,0:T(2,128)(2,1)}), bf16[128,2,128]{2,1,0:T(2,128)(2,1)S(1)}, u32[]{:S(2)}, u32[]{:S(2)}) %all-to-all-start.3) | async-done | bytes 65568 | tf_op jit(solution)/shard_map/all_to_all | solution.py:67
  55.0 3.9 %all-to-all-start.1 = ((bf16[32,4,32]{2,1,0:T(4,128)(2,1)}), bf16[32,4,32]{2,1,0:T(4,128)(2,1)S(1)}, u32[]{:S(2)}, u32[]{:S(2)}) async-start(bf16[32,4,32]{2,1,0:T(4,128)(2,1)} %fusion.38), calls=%async_computation.1 | async-start | bytes 65536 | tf_op jit(solution)/shard_map/all_to_all | solution.py:63
  60.3 11.9 %all-to-all-done.1 = bf16[32,4,32]{2,1,0:T(4,128)(2,1)S(1)} async-done(((bf16[32,4,32]{2,1,0:T(4,128)(2,1)}), bf16[32,4,32]{2,1,0:T(4,128)(2,1)S(1)}, u32[]{:S(2)}, u32[]{:S(2)}) %all-to-all-start.1) | async-done | bytes 8224 | tf_op jit(solution)/shard_map/all_to_all | solution.py:63
  72.2 26.0 %all-gather.25.cloned.1.call-done = bf16[2048,2048]{1,0:T(8,128)(2,1)} async-done(((bf16[64,2048]{1,0:T(8,128)(2,1)}), bf16[2048,2048]{1,0:T(8,128)(2,1)}) %all-gather.25.cloned.1.call-update) | async-done | bytes 8388624 | tf_op jit(solution)/shard_map/all_gather | solution.py:52
  101.8 5.8 %all-to-all-start.2 = ((bf16[8,4,2048]{2,1,0:T(4,128)(2,1)}), bf16[8,4,2048]{2,1,0:T(4,128)(2,1)S(1)}, u32[]{:S(2)}, u32[]{:S(2)}) async-start(bf16[8,4,2048]{2,1,0:T(4,128)(2,1)} %broadcast_in_dim.20), calls=%async_computation.2 | async-start | bytes 262144 | tf_op jit(solution)/shard_map/all_to_all | solution.py:24
  107.6 6.0 %fusion.84 = (bf16[32,32,2048]{2,1,0:T(8,128)(2,1)}, bf16[32,32,2048]{2,1,0:T(8,128)(2,1)}) fusion(bf16[32,64,2048]{2,1,0:T(8,128)(2,1)} %bitcast.128), kind=kLoop, calls=%fused_computation.149 | loop fusion | bytes 16777216 | tf_op jit(solution)/shard_map/slice | solution.py:53
  118.3 5.9 %all-gather.12 = bf16[2,4,1024]{2,1,0:T(4,128)(2,1)S(1)} all-gather(bf16[1,4,1024]{2,1,0:T(4,128)(2,1)S(1)} %fusion.9), channel_id=4, replica_groups=mesh['x'=4,'core'=2,'z'=16,'yl'=2,'mp'=2] {'mp'}, dimensions={0}, use_global_device_ids=true | all-gather | bytes 24576 | tf_op jit(solution)/shard_map/all_gather | solution.py:76
  125.6 5.7 %all-to-all-start.4 = ((bf16[8,4,2048]{2,1,0:T(4,128)(2,1)}), bf16[8,4,2048]{2,1,0:T(4,128)(2,1)S(1)}, u32[]{:S(2)}, u32[]{:S(2)}) async-start(bf16[8,4,2048]{2,1,0:T(4,128)(2,1)} %broadcast_in_dim.21), calls=%async_computation.4 | async-start | bytes 262144 | tf_op jit(solution)/shard_map/all_to_all | solution.py:24
  131.9 4.8 %all-to-all-done.4 = bf16[8,4,2048]{2,1,0:T(4,128)(2,1)S(1)} async-done(((bf16[8,4,2048]{2,1,0:T(4,128)(2,1)}), bf16[8,4,2048]{2,1,0:T(4,128)(2,1)S(1)}, u32[]{:S(2)}, u32[]{:S(2)}) %all-to-all-start.4) | async-done | bytes 131104 | tf_op jit(solution)/shard_map/all_to_all | solution.py:24
  140.4 5.9 %all-gather.13 = bf16[2,4,1024]{2,1,0:T(4,128)(2,1)S(1)} all-gather(bf16[1,4,1024]{2,1,0:T(4,128)(2,1)S(1)} %fusion.10), channel_id=5, replica_groups=mesh['x'=4,'core'=2,'z'=16,'yl'=2,'mp'=2] {'mp'}, dimensions={0}, use_global_device_ids=true | all-gather | bytes 24576 | tf_op jit(solution)/shard_map/all_gather | solution.py:76
  147.1 10.6 %all_to_all.70 = bf16[8,4,2048]{2,1,0:T(4,128)(2,1)S(1)} all-to-all(bf16[8,4,2048]{2,1,0:T(4,128)(2,1)S(1)} %broadcast_in_dim.22), channel_id=1, replica_groups=mesh['x'=4,'core'=2,'z'=16,'yl'=2,'mp'=2] {'x','yl'}, dimensions={0} | all-to-all | bytes 262144 | tf_op jit(solution)/shard_map/all_to_all | solution.py:24
  159.1 6.0 %all-gather.14 = bf16[2,4,1024]{2,1,0:T(4,128)(2,1)S(1)} all-gather(bf16[1,4,1024]{2,1,0:T(4,128)(2,1)S(1)} %fusion.11), channel_id=6, replica_groups=mesh['x'=4,'core'=2,'z'=16,'yl'=2,'mp'=2] {'mp'}, dimensions={0}, use_global_device_ids=true | all-gather | bytes 24576 | tf_op jit(solution)/shard_map/all_gather | solution.py:76
  166.0 9.1 %all_to_all.71 = bf16[8,4,2048]{2,1,0:T(4,128)(2,1)S(1)} all-to-all(bf16[8,4,2048]{2,1,0:T(4,128)(2,1)S(1)} %broadcast_in_dim.23), channel_id=1, replica_groups=mesh['x'=4,'core'=2,'z'=16,'yl'=2,'mp'=2] {'x','yl'}, dimensions={0} | all-to-all | bytes 262144 | tf_op jit(solution)/shard_map/all_to_all | solution.py:24
  176.4 5.9 %all-gather.15 = bf16[2,4,1024]{2,1,0:T(4,128)(2,1)S(1)} all-gather(bf16[1,4,1024]{2,1,0:T(4,128)(2,1)S(1)} %fusion.12), channel_id=7, replica_groups=mesh['x'=4,'core'=2,'z'=16,'yl'=2,'mp'=2] {'mp'}, dimensions={0}, use_global_device_ids=true | all-gather | bytes 24576 | tf_op jit(solution)/shard_map/all_gather | solution.py:76
  183.1 9.2 %all_to_all.72 = bf16[8,4,2048]{2,1,0:T(4,128)(2,1)S(1)} all-to-all(bf16[8,4,2048]{2,1,0:T(4,128)(2,1)S(1)} %broadcast_in_dim.24), channel_id=1, replica_groups=mesh['x'=4,'core'=2,'z'=16,'yl'=2,'mp'=2] {'x','yl'}, dimensions={0} | all-to-all | bytes 262144 | tf_op jit(solution)/shard_map/all_to_all | solution.py:24
  193.6 5.9 %all-gather.16 = bf16[2,4,1024]{2,1,0:T(4,128)(2,1)S(1)} all-gather(bf16[1,4,1024]{2,1,0:T(4,128)(2,1)S(1)} %fusion.13), channel_id=8, replica_groups=mesh['x'=4,'core'=2,'z'=16,'yl'=2,'mp'=2] {'mp'}, dimensions={0}, use_global_device_ids=true | all-gather | bytes 24576 | tf_op jit(solution)/shard_map/all_gather | solution.py:76
  200.3 9.1 %all_to_all.73 = bf16[8,4,2048]{2,1,0:T(4,128)(2,1)S(1)} all-to-all(bf16[8,4,2048]{2,1,0:T(4,128)(2,1)S(1)} %broadcast_in_dim.25), channel_id=1, replica_groups=mesh['x'=4,'core'=2,'z'=16,'yl'=2,'mp'=2] {'x','yl'}, dimensions={0} | all-to-all | bytes 262144 | tf_op jit(solution)/shard_map/all_to_all | solution.py:24
  215.4 5.9 %all-gather.17 = bf16[2,4,1024]{2,1,0:T(4,128)(2,1)S(1)} all-gather(bf16[1,4,1024]{2,1,0:T(4,128)(2,1)S(1)} %fusion.14), channel_id=10, replica_groups=mesh['x'=4,'core'=2,'z'=16,'yl'=2,'mp'=2] {'mp'}, dimensions={0}, use_global_device_ids=true | all-gather | bytes 24576 | tf_op jit(solution)/shard_map/all_gather | solution.py:76
  222.8 4.3 %all-to-all-start.9 = ((bf16[8,4,2048]{2,1,0:T(4,128)(2,1)}), bf16[8,4,2048]{2,1,0:T(4,128)(2,1)S(1)}, u32[]{:S(2)}, u32[]{:S(2)}) async-start(bf16[8,4,2048]{2,1,0:T(4,128)(2,1)} %broadcast_in_dim.26), calls=%async_computation.9 | async-start | bytes 262144 | tf_op jit(solution)/shard_map/all_to_all | solution.py:24
  227.2 5.2 %all-to-all-done.9 = bf16[8,4,2048]{2,1,0:T(4,128)(2,1)S(1)} async-done(((bf16[8,4,2048]{2,1,0:T(4,128)(2,1)}), bf16[8,4,2048]{2,1,0:T(4,128)(2,1)S(1)}, u32[]{:S(2)}, u32[]{:S(2)}) %all-to-all-start.9) | async-done | bytes 131104 | tf_op jit(solution)/shard_map/all_to_all | solution.py:24
  236.2 5.9 %all-gather.18 = bf16[2,4,1024]{2,1,0:T(4,128)(2,1)S(1)} all-gather(bf16[1,4,1024]{2,1,0:T(4,128)(2,1)S(1)} %fusion.15), channel_id=12, replica_groups=mesh['x'=4,'core'=2,'z'=16,'yl'=2,'mp'=2] {'mp'}, dimensions={0}, use_global_device_ids=true | all-gather | bytes 24576 | tf_op jit(solution)/shard_map/all_gather | solution.py:76
  243.5 4.3 %all-to-all-start.11 = ((bf16[8,4,2048]{2,1,0:T(4,128)(2,1)}), bf16[8,4,2048]{2,1,0:T(4,128)(2,1)S(1)}, u32[]{:S(2)}, u32[]{:S(2)}) async-start(bf16[8,4,2048]{2,1,0:T(4,128)(2,1)} %broadcast_in_dim.28), calls=%async_computation.11 | async-start | bytes 262144 | tf_op jit(solution)/shard_map/all_to_all | solution.py:24
  248.2 5.0 %all-to-all-done.11 = bf16[8,4,2048]{2,1,0:T(4,128)(2,1)S(1)} async-done(((bf16[8,4,2048]{2,1,0:T(4,128)(2,1)}), bf16[8,4,2048]{2,1,0:T(4,128)(2,1)S(1)}, u32[]{:S(2)}, u32[]{:S(2)}) %all-to-all-start.11) | async-done | bytes 131104 | tf_op jit(solution)/shard_map/all_to_all | solution.py:24
  253.2 22.1 %all_to_all.74 = bf16[32,7,128]{2,1,0:T(8,128)(2,1)S(1)} all-to-all(bf16[32,7,128]{2,1,0:T(8,128)(2,1)S(1)} %reshape.177), channel_id=1, replica_groups=mesh['x'=4,'core'=2,'z'=16,'yl'=2,'mp'=2] {'z','core'}, dimensions={0} | all-to-all | bytes 114688 | tf_op jit(solution)/shard_map/all_to_all | solution.py:93
  279.8 18.1 %all-to-all-done.10 = bf16[16,4,2048]{2,1,0:T(4,128)(2,1)S(1)} async-done(((bf16[16,4,2048]{2,1,0:T(4,128)(2,1)}), bf16[16,4,2048]{2,1,0:T(4,128)(2,1)S(1)}, u32[]{:S(2)}, u32[]{:S(2)}) %all-to-all-start.10) | async-done | bytes 262176 | tf_op jit(solution)/shard_map/all_to_all | solution.py:24
  298.7 5.9 %all-to-all-start.12 = ((bf16[16,4,2048]{2,1,0:T(4,128)(2,1)}), bf16[16,4,2048]{2,1,0:T(4,128)(2,1)S(1)}, u32[]{:S(2)}, u32[]{:S(2)}) async-start(bf16[16,4,2048]{2,1,0:T(4,128)(2,1)} %broadcast_in_dim.29), calls=%async_computation.12 | async-start | bytes 524288 | tf_op jit(solution)/shard_map/all_to_all | solution.py:24
  305.6 3.7 %convolution_bitcast_fusion = f32[1,1,32,2048]{3,2,1,0:T(8,128)} fusion(bf16[8,128,32]{1,2,0:T(8,128)(2,1)S(1)} %rev.6, bf16[8,128,2048]{2,1,0:T(8,128)(2,1)} %all-gather.23.cloned.1.call-done), kind=kOutput, calls=%fused_computation.10 | convolution fusion | flops 134217728 | bytes 4521984 | tf_op jit(solution)/shard_map/dot_general | solution.py:36
  313.2 9.9 %all-to-all-done.12 = bf16[16,4,2048]{2,1,0:T(4,128)(2,1)S(1)} async-done(((bf16[16,4,2048]{2,1,0:T(4,128)(2,1)}), bf16[16,4,2048]{2,1,0:T(4,128)(2,1)S(1)}, u32[]{:S(2)}, u32[]{:S(2)}) %all-to-all-start.12) | async-done | bytes 262176 | tf_op jit(solution)/shard_map/all_to_all | solution.py:24
  326.8 4.0 %reshape.111 = bf16[32,6,4,2048]{3,2,1,0:T(4,128)(2,1)S(1)} reshape(bf16[768,2048]{1,0:T(8,128)(2,1)} %all-gather.27.cloned.1.call-done) | data formatting | bytes 6291456 | tf_op jit(solution)/shard_map/reshape | solution.py:84
  (144 shorter events, 67.9 us)
Async XLA Ops:
  8.0 90.2 %all-gather.25.cloned.1.call-start = ((), (), s32[]{:S(2)}) async-start(), calls=%async_computation.15 | async-start | bytes 8650752 | tf_op jit(solution)/shard_map/all_gather | solution.py:52
  11.3 9.9 %all-to-all-start = ((bf16[8,128,32]{1,2,0:T(8,128)(2,1)}), bf16[8,128,32]{1,2,0:T(8,128)(2,1)S(1)}, u32[]{:S(2)}, u32[]{:S(2)}) async-start(bf16[8,128,32]{1,2,0:T(8,128)(2,1)} %bitcast.3), calls=%async_computation | async-start | bytes 131072 | tf_op jit(solution)/shard_map/all_to_all | solution.py:57
  21.3 33.7 %all-to-all-start.3 = ((bf16[128,2,128]{2,1,0:T(2,128)(2,1)}), bf16[128,2,128]{2,1,0:T(2,128)(2,1)S(1)}, u32[]{:S(2)}, u32[]{:S(2)}) async-start(bf16[128,2,128]{2,1,0:T(2,128)(2,1)} %reshape.109), calls=%async_computation.3 | async-start | bytes 131072 | tf_op jit(solution)/shard_map/all_to_all | solution.py:67
  55.0 17.2 %all-to-all-start.1 = ((bf16[32,4,32]{2,1,0:T(4,128)(2,1)}), bf16[32,4,32]{2,1,0:T(4,128)(2,1)S(1)}, u32[]{:S(2)}, u32[]{:S(2)}) async-start(bf16[32,4,32]{2,1,0:T(4,128)(2,1)} %fusion.38), calls=%async_computation.1 | async-start | bytes 65536 | tf_op jit(solution)/shard_map/all_to_all | solution.py:63
  101.8 11.9 %all-to-all-start.2 = ((bf16[8,4,2048]{2,1,0:T(4,128)(2,1)}), bf16[8,4,2048]{2,1,0:T(4,128)(2,1)S(1)}, u32[]{:S(2)}, u32[]{:S(2)}) async-start(bf16[8,4,2048]{2,1,0:T(4,128)(2,1)} %broadcast_in_dim.20), calls=%async_computation.2 | async-start | bytes 262144 | tf_op jit(solution)/shard_map/all_to_all | solution.py:24
  113.7 10.6 %copy-start = (bf16[32,32,2048]{2,1,0:T(8,128)(2,1)S(1)}, bf16[32,32,2048]{2,1,0:T(8,128)(2,1)}, u32[]{:S(2)}) copy-start(bf16[32,32,2048]{2,1,0:T(8,128)(2,1)} %get-tuple-element.18) | copy-start | bytes 12582916
  125.6 11.1 %all-to-all-start.4 = ((bf16[8,4,2048]{2,1,0:T(4,128)(2,1)}), bf16[8,4,2048]{2,1,0:T(4,128)(2,1)S(1)}, u32[]{:S(2)}, u32[]{:S(2)}) async-start(bf16[8,4,2048]{2,1,0:T(4,128)(2,1)} %broadcast_in_dim.21), calls=%async_computation.4 | async-start | bytes 262144 | tf_op jit(solution)/shard_map/all_to_all | solution.py:24
  131.3 174.2 %all-gather.23.cloned.1.call-start = ((), (), s32[]{:S(2)}) async-start(), calls=%async_computation.14 | async-start | bytes 4718592 | tf_op jit(solution)/shard_map/all_gather | solution.py:55
  131.9 194.9 %all-gather.27.cloned.1.call-start = ((), (), s32[]{:S(2)}) async-start(), calls=%async_computation.16 | async-start | bytes 3244032 | tf_op jit(solution)/shard_map/all_gather | solution.py:84
  136.7 9.7 %copy-start.1 = (bf16[32,32,2048]{2,1,0:T(8,128)(2,1)S(1)}, bf16[32,32,2048]{2,1,0:T(8,128)(2,1)}, u32[]{:S(2)}) copy-start(bf16[32,32,2048]{2,1,0:T(8,128)(2,1)} %get-tuple-element.18) | copy-start | bytes 12582916
  136.9 21.0 %copy-start.4 = (bf16[32,32,2048]{2,1,0:T(8,128)(2,1)S(1)}, bf16[32,32,2048]{2,1,0:T(8,128)(2,1)}, u32[]{:S(2)}) copy-start(bf16[32,32,2048]{2,1,0:T(8,128)(2,1)} %get-tuple-element.17) | copy-start | bytes 12582916
  211.9 9.5 %copy-start.2 = (bf16[32,32,2048]{2,1,0:T(8,128)(2,1)S(1)}, bf16[32,32,2048]{2,1,0:T(8,128)(2,1)}, u32[]{:S(2)}) copy-start(bf16[32,32,2048]{2,1,0:T(8,128)(2,1)} %get-tuple-element.18) | copy-start | bytes 12582916
  222.8 9.7 %all-to-all-start.9 = ((bf16[8,4,2048]{2,1,0:T(4,128)(2,1)}), bf16[8,4,2048]{2,1,0:T(4,128)(2,1)S(1)}, u32[]{:S(2)}, u32[]{:S(2)}) async-start(bf16[8,4,2048]{2,1,0:T(4,128)(2,1)} %broadcast_in_dim.26), calls=%async_computation.9 | async-start | bytes 262144 | tf_op jit(solution)/shard_map/all_to_all | solution.py:24
  232.5 9.6 %copy-start.3 = (bf16[32,32,2048]{2,1,0:T(8,128)(2,1)S(1)}, bf16[32,32,2048]{2,1,0:T(8,128)(2,1)}, u32[]{:S(2)}) copy-start(bf16[32,32,2048]{2,1,0:T(8,128)(2,1)} %get-tuple-element.18) | copy-start | bytes 12582916
  243.5 9.7 %all-to-all-start.11 = ((bf16[8,4,2048]{2,1,0:T(4,128)(2,1)}), bf16[8,4,2048]{2,1,0:T(4,128)(2,1)S(1)}, u32[]{:S(2)}, u32[]{:S(2)}) async-start(bf16[8,4,2048]{2,1,0:T(4,128)(2,1)} %broadcast_in_dim.28), calls=%async_computation.11 | async-start | bytes 262144 | tf_op jit(solution)/shard_map/all_to_all | solution.py:24
  276.1 21.8 %all-to-all-start.10 = ((bf16[16,4,2048]{2,1,0:T(4,128)(2,1)}), bf16[16,4,2048]{2,1,0:T(4,128)(2,1)S(1)}, u32[]{:S(2)}, u32[]{:S(2)}) async-start(bf16[16,4,2048]{2,1,0:T(4,128)(2,1)} %broadcast_in_dim.27), calls=%async_computation.10 | async-start | bytes 524288 | tf_op jit(solution)/shard_map/all_to_all | solution.py:24
  298.7 24.4 %all-to-all-start.12 = ((bf16[16,4,2048]{2,1,0:T(4,128)(2,1)}), bf16[16,4,2048]{2,1,0:T(4,128)(2,1)S(1)}, u32[]{:S(2)}, u32[]{:S(2)}) async-start(bf16[16,4,2048]{2,1,0:T(4,128)(2,1)} %broadcast_in_dim.29), calls=%async_computation.12 | async-start | bytes 524288 | tf_op jit(solution)/shard_map/all_to_all | solution.py:24
  312.1 14.6 %copy-start.5 = (bf16[32,1,4,2048]{3,2,0,1:T(4,128)(2,1)}, bf16[32,1,4,2048]{3,2,0,1:T(4,128)(2,1)S(1)}, u32[]{:S(2)}) copy-start(bf16[32,1,4,2048]{3,2,0,1:T(4,128)(2,1)S(1)} %reshape.112) | copy-start | bytes 1572868
  330.8 1.8 copy-start.9
  332.5 1.0 copy-start.7
  332.6 1.9 copy-start.6
  332.6 1.9 copy-start.8
Sparse Core Ops, SparseCore 0:
  11.5 86.6 all-gather.24
Sparse Core Ops, SparseCore 1:
  133.9 37.3 all-gather.22
  211.6 69.0 all-gather.26
